TPU v7x, 256 devices: a whole 4x4x8 slice. The times are simulated.
256 devices in a mesh: blk: 32 (over x, z_lo, y), grp: 8 (over z_hi, core).
Axes of the slice: x: 4, y: 4, z: 8 (z_hi: 4, z_lo: 2; z = z_hi * 2 + z_lo), core: 2. Of those that a mesh axis runs over, the one named last changes fastest.
Arguments:
- points: bfloat16 [64, 32768], P(None, ('blk', 'grp')), may hold values from -6 to 6
- right_side: float32 [16, 32768], P(None, ('blk', 'grp')), may hold values from -18 to 18
- lengthscale: float32 [1], replicated, may hold values from 2.7305508 to 3.3440894
- outputscale: float32 [1], replicated, may hold values from 0.6 to 1.6
- noise_level: float32 [1], replicated, may hold values from 0.4 to 1
Outputs:
- solution: float32 [16, 32768], P(None, ('blk', 'grp'))
- residual: float32 [16, 32768], P(None, ('blk', 'grp'))
- gradient: float32 [3], replicated
All inputs are finite; a program needn't handle non-finite values.
Results may differ from a plain program's by a relative error of at most 0.001.
The roundings to bfloat16 on the way count: a program that leaves them out, or rounds other values in their place, can miss the bound.
Values may be sent and summed in bfloat16 or wider, within the bound.
A program may use at most 64 MiB of HBM per device.

v0:
```python
import functools
import math

import jax
import jax.numpy as jnp
from jax import lax
from jax.sharding import Mesh
from jax.sharding import PartitionSpec as P

ITERS = 2
GRP = ("grp_0", "grp_1")
BLK = ("blk_0", "blk_1", "blk_2")
BLK_GRP = ("blk_0", "blk_1", "blk_2", "grp_0", "grp_1")


def from_everyone(x, axis):
    copies = jnp.broadcast_to(x, (lax.axis_size(axis), *x.shape))
    return lax.all_to_all(copies, axis, split_axis=0, concat_axis=0, tiled=True)


def in_order(tiles, dim):
    lengths = list(tiles.shape[1:])
    lengths[dim] *= tiles.shape[0]
    return jnp.moveaxis(tiles, 0, dim).reshape(lengths)


def gather_directly(x, axis, dim):
    tiles = from_everyone(x, axis)
    return in_order(tiles, dim)


def shifted(x, axis, by):
    size = lax.axis_size(axis)
    return lax.ppermute(x, axis, [(i, (i + by) % size) for i in range(size)])


def cut_along(x, dim, size):
    before, after = (x.shape[:dim], x.shape[dim + 1 :])
    return jnp.moveaxis(x.reshape(*before, size, -1, *after), dim, 0)


def summed_on_arrival(x, axis, dim):
    tiles = cut_along(x, dim, lax.axis_size(axis))
    arrived = lax.all_to_all(tiles, axis, split_axis=0, concat_axis=0, tiled=True)
    return arrived.sum(axis=0)


def one_axis_at_a_time(x, axes):
    return functools.reduce(lax.psum, axes, x)


def kernel_tiles(own_points, own_squares, tile_points, scale_len, with_grad):
    tile_squares = jnp.sum(jnp.square(tile_points.astype(jnp.float32)), axis=0)
    inner_prod = lax.dot_general(
        own_points, tile_points, (((0,), (0,)), ((), ())), preferred_element_type=jnp.float32
    )
    distance = jnp.maximum(own_squares[:, None] + tile_squares[None, :] - 2.0 * inner_prod, 0.0)
    radius = jnp.sqrt(5.0 * distance) / scale_len
    damping = jnp.exp(-radius)
    tiles = [((1.0 + radius + radius * radius / 3.0) * damping).astype(jnp.bfloat16)]
    if with_grad:
        tiles.append(
            (radius * radius * (1.0 + radius) * damping / (3.0 * scale_len)).astype(jnp.bfloat16)
        )
    return tiles


def apply_columns(tile_vectors, single):
    return lax.dot_general(
        tile_vectors, single, (((1,), (1,)), ((), ())), preferred_element_type=jnp.float32
    )


def apply_rows(own_vectors, single):
    return lax.dot_general(
        own_vectors, single, (((1,), (0,)), ((), ())), preferred_element_type=jnp.float32
    )


def sweep(own_side, visitor, scale_len, with_grad, forward_sum, backward_sum):
    own_points, own_squares, own_vectors = own_side
    visit_points, visit_vectors = visitor
    column_count = visit_points.shape[1]
    block_width = math.gcd(column_count, max(512, own_points.shape[1]))

    def one_block(block_index, carried):
        forward_sum, backward_sum = carried
        offset = block_index * block_width
        tile_points = lax.dynamic_slice_in_dim(visit_points, offset, block_width, 1)
        tile_vectors = lax.dynamic_slice_in_dim(visit_vectors, offset, block_width, 1)
        tiles = kernel_tiles(own_points, own_squares, tile_points, scale_len, with_grad)
        forward_sum = forward_sum + jnp.concatenate(
            [apply_columns(tile_vectors, single) for single in tiles], axis=0
        )
        if backward_sum is not None:
            previous = lax.dynamic_slice_in_dim(backward_sum, offset, block_width, 1)
            update = jnp.concatenate([apply_rows(own_vectors, single) for single in tiles], axis=0)
            backward_sum = lax.dynamic_update_slice_in_dim(
                backward_sum, previous + update, offset, 1
            )
        return (forward_sum, backward_sum)

    return lax.fori_loop(0, column_count // block_width, one_block, (forward_sum, backward_sum))


def local(points, right_side, lengthscale, outputscale, noise_level):
    scale_len = lengthscale[0]
    amplitude = outputscale[0]
    jitter = noise_level[0]
    squares = jnp.sum(jnp.square(points.astype(jnp.float32)), axis=0)
    column_count = right_side.shape[0]
    own_rows = points.shape[1]
    group_points = gather_directly(points, GRP, 1)

    def kernel_product(vectors, with_grad):
        rounded = vectors.astype(jnp.bfloat16)
        own_side = (points, squares, rounded)
        out_rows = column_count * (2 if with_grad else 1)
        empty = jnp.zeros((out_rows, own_rows), jnp.float32)
        group_vectors = gather_directly(rounded, GRP, 1)
        forward_sum, unused = sweep(
            own_side, (group_points, group_vectors), scale_len, with_grad, empty, None
        )
        half_blocks = lax.axis_size(BLK) // 2
        backward_sum = jnp.zeros((out_rows, group_points.shape[1]), jnp.float32)

        def visit_turn(turn_index, carried):
            visit_points, visit_vectors, backward_sum, forward_sum = carried
            visit_points, visit_vectors = shifted((visit_points, visit_vectors), BLK, 1)
            backward_sum = shifted(backward_sum, BLK, 1)
            forward_sum, backward_sum = sweep(
                own_side,
                (visit_points, visit_vectors),
                scale_len,
                with_grad,
                forward_sum,
                backward_sum,
            )
            return (visit_points, visit_vectors, backward_sum, forward_sum)

        carried = lax.fori_loop(
            0, half_blocks - 1, visit_turn, (group_points, group_vectors, backward_sum, forward_sum)
        )
        visit_points, visit_vectors, backward_sum, forward_sum = carried
        returned = shifted(backward_sum, BLK, 1 - half_blocks)
        far_points, far_vectors = shifted((visit_points, visit_vectors), BLK, 1)
        forward_sum, unused = sweep(
            own_side, (far_points, far_vectors), scale_len, with_grad, forward_sum, None
        )
        return forward_sum + summed_on_arrival(returned, GRP, 1)

    def system(vectors):
        return amplitude * kernel_product(vectors, False) + jitter * vectors

    solution = jnp.zeros_like(right_side)
    residual = right_side
    direction = right_side
    norm_now = one_axis_at_a_time(jnp.sum(residual * residual, axis=1), BLK_GRP)
    applied = system(direction)
    curvature = one_axis_at_a_time(jnp.sum(direction * applied, axis=1), BLK_GRP)
    for iteration in range(ITERS):
        if iteration > 0:
            applied = system(direction)
            curvature = one_axis_at_a_time(jnp.sum(direction * applied, axis=1), BLK_GRP)
        step_size = norm_now / curvature
        solution = solution + step_size[:, None] * direction
        residual = residual - step_size[:, None] * applied
        if iteration + 1 < ITERS:
            norm_next = one_axis_at_a_time(jnp.sum(residual * residual, axis=1), BLK_GRP)
            direction = residual + (norm_next / norm_now)[:, None] * direction
            norm_now = norm_next
    products_out = kernel_product(solution, True)
    kernel_part = products_out[:column_count]
    slope_part = products_out[column_count:]
    left_side = jnp.concatenate([solution[:1], right_side[1:]], axis=0)
    weights = jnp.where(
        lax.iota(jnp.int32, column_count) == 0, 1.0, -1.0 / (column_count - 1)
    ).astype(jnp.float32)[:, None]
    local_terms = jnp.stack(
        [
            jnp.sum(weights * left_side * amplitude * slope_part),
            jnp.sum(weights * left_side * kernel_part),
            jnp.sum(weights * left_side * solution),
        ]
    )
    total_points = own_rows * lax.axis_size(BLK) * lax.axis_size(GRP)
    gradient = 0.5 * one_axis_at_a_time(local_terms, BLK_GRP) / total_points
    return (solution, residual, gradient)


def solution(mesh):
    split = Mesh(mesh.devices.reshape(4, 2, 4, 4, 2), ("blk_0", "blk_1", "blk_2", "grp_0", "grp_1"))
    return jax.shard_map(
        local,
        mesh=split,
        in_specs=(P(None, BLK_GRP), P(None, BLK_GRP), P(), P(), P()),
        out_specs=(P(None, BLK_GRP), P(None, BLK_GRP), P()),
        check_vma=False,
    )
```

profile of v0, /device:TPU:1, one launch (start us, length us, event | category | flops | bytes accessed | tf_op | source)
XLA Modules:
  0.0 911.7 jit_solution(8373113232517858535)
XLA Ops:
  1.3 17.1 %all_to_all.35 = bf16[8,16,128]{2,1,0:T(8,128)(2,1)S(1)} all-to-all(bf16[8,16,128]{2,1,0:T(8,128)(2,1)S(1)} %broadcast_in_dim.87), channel_id=1, replica_groups=mesh['blk_0'=4,'blk_1'=2,'blk_2'=4,'grp_0'=4,'grp_1'=2] {'grp_0','grp_1'}, dimensions={0} | all-to-all | bytes 65536 | tf_op jit(solution)/shard_map/all_to_all | solution.py:18
  33.7 187.4 %while.182 = (s32[]{:T(128)}, bf16[64,1024]{1,0:T(8,128)(2,1)S(1)}, bf16[16,1024]{1,0:T(8,128)(2,1)S(1)}, f32[16,1024]{1,0:T(8,128)S(1)}, f32[16,128]{1,0:T(8,12...) while((s32[]{:T(128)}, bf16[64,1024]{1,0:T(8,128)(2,1)S(1)}, ...), condition=%wide.region_14.0_spmd, body=%wide.region_10.0_spmd.sunk | while | flops 13542920 | bytes 2024500 | solution.py:141
  143.0 10.4 %collective-permute-done.7 = bf16[16,1024]{1,0:T(8,128)(2,1)S(1)} collective-permute-done((bf16[16,1024]{1,0:T(8,128)(2,1)S(1)}, bf16[16,1024]{1,0:T(8,128)(2,1)S(1)}, u32[]{:S(2)}, u32[]{:S(2)}) %collective-permute-start.7) | collective-permute-done | bytes 32800 | tf_op jit(solution)/shard_map/while/body/eval_jaxpr/ppermute | solution.py:34
  156.4 11.5 %collective-permute-done.7 = bf16[16,1024]{1,0:T(8,128)(2,1)S(1)} collective-permute-done((bf16[16,1024]{1,0:T(8,128)(2,1)S(1)}, bf16[16,1024]{1,0:T(8,128)(2,1)S(1)}, u32[]{:S(2)}, u32[]{:S(2)}) %collective-permute-start.7) | collective-permute-done | bytes 32800 | tf_op jit(solution)/shard_map/while/body/eval_jaxpr/ppermute | solution.py:34
  170.9 10.6 %collective-permute-done.7 = bf16[16,1024]{1,0:T(8,128)(2,1)S(1)} collective-permute-done((bf16[16,1024]{1,0:T(8,128)(2,1)S(1)}, bf16[16,1024]{1,0:T(8,128)(2,1)S(1)}, u32[]{:S(2)}, u32[]{:S(2)}) %collective-permute-start.7) | collective-permute-done | bytes 32800 | tf_op jit(solution)/shard_map/while/body/eval_jaxpr/ppermute | solution.py:34
  184.6 9.8 %collective-permute-done.7 = bf16[16,1024]{1,0:T(8,128)(2,1)S(1)} collective-permute-done((bf16[16,1024]{1,0:T(8,128)(2,1)S(1)}, bf16[16,1024]{1,0:T(8,128)(2,1)S(1)}, u32[]{:S(2)}, u32[]{:S(2)}) %collective-permute-start.7) | collective-permute-done | bytes 32800 | tf_op jit(solution)/shard_map/while/body/eval_jaxpr/ppermute | solution.py:34
  228.0 22.1 %all-to-all-start.2 = ((f32[8,16,128]{2,1,0:T(8,128)}), f32[8,16,128]{2,1,0:T(8,128)S(1)}, u32[]{:S(2)}, u32[]{:S(2)}) async-start(f32[8,16,128]{2,1,0:T(8,128)} %copy.10), calls=%async_computation.2 | async-start | bytes 131072 | tf_op jit(solution)/shard_map/all_to_all | solution.py:44
  285.5 9.7 %all-reduce.3 = (f32[16]{0:T(128)S(1)}, f32[16]{0:T(128)S(1)}) all-reduce(f32[16]{0:T(128)S(1)} %get-tuple-element.1808, f32[16]{0:T(128)S(1)} %get-tuple-element.1809), channel_id=1, replica_groups=mesh['blk_0'=4,'blk_1'=2,'blk_2'=4,'grp_0'=4,'grp_1'=2] {'grp_1'}, use_global_device_ids=true, to_apply=%region_5.0 | all-reduce | flops 32 | bytes 256 | tf_op jit(solution)/shard_map/psum | solution.py:49
  345.5 188.5 %while.185 = (s32[]{:T(128)}, bf16[64,1024]{1,0:T(8,128)(2,1)S(1)}, bf16[16,1024]{1,0:T(8,128)(2,1)S(1)}, f32[16,1024]{1,0:T(8,128)S(1)}, f32[16,128]{1,0:T(8,12...) while((s32[]{:T(128)}, bf16[64,1024]{1,0:T(8,128)(2,1)S(1)}, ...), condition=%wide.region_38.0_spmd, body=%wide.region_34.0_spmd.sunk | while | flops 13542920 | bytes 2024500 | solution.py:141
  467.9 10.4 %collective-permute-done.4 = bf16[16,1024]{1,0:T(8,128)(2,1)S(1)} collective-permute-done((bf16[16,1024]{1,0:T(8,128)(2,1)S(1)}, bf16[16,1024]{1,0:T(8,128)(2,1)S(1)}, u32[]{:S(2)}, u32[]{:S(2)}) %collective-permute-start.4) | collective-permute-done | bytes 32800 | tf_op jit(solution)/shard_map/while/body/eval_jaxpr/ppermute | solution.py:34
  481.3 11.5 %collective-permute-done.4 = bf16[16,1024]{1,0:T(8,128)(2,1)S(1)} collective-permute-done((bf16[16,1024]{1,0:T(8,128)(2,1)S(1)}, bf16[16,1024]{1,0:T(8,128)(2,1)S(1)}, u32[]{:S(2)}, u32[]{:S(2)}) %collective-permute-start.4) | collective-permute-done | bytes 32800 | tf_op jit(solution)/shard_map/while/body/eval_jaxpr/ppermute | solution.py:34
  495.8 10.6 %collective-permute-done.4 = bf16[16,1024]{1,0:T(8,128)(2,1)S(1)} collective-permute-done((bf16[16,1024]{1,0:T(8,128)(2,1)S(1)}, bf16[16,1024]{1,0:T(8,128)(2,1)S(1)}, u32[]{:S(2)}, u32[]{:S(2)}) %collective-permute-start.4) | collective-permute-done | bytes 32800 | tf_op jit(solution)/shard_map/while/body/eval_jaxpr/ppermute | solution.py:34
  509.5 9.8 %collective-permute-done.4 = bf16[16,1024]{1,0:T(8,128)(2,1)S(1)} collective-permute-done((bf16[16,1024]{1,0:T(8,128)(2,1)S(1)}, bf16[16,1024]{1,0:T(8,128)(2,1)S(1)}, u32[]{:S(2)}, u32[]{:S(2)}) %collective-permute-start.4) | collective-permute-done | bytes 32800 | tf_op jit(solution)/shard_map/while/body/eval_jaxpr/ppermute | solution.py:34
  541.2 20.9 %all-to-all-start.4 = ((f32[8,16,128]{2,1,0:T(8,128)}), f32[8,16,128]{2,1,0:T(8,128)S(1)}, u32[]{:S(2)}, u32[]{:S(2)}) async-start(f32[8,16,128]{2,1,0:T(8,128)} %copy.12), calls=%async_computation.4 | async-start | bytes 131072 | tf_op jit(solution)/shard_map/all_to_all | solution.py:44
  596.8 9.7 %psum.194 = f32[16]{0:T(128)S(1)} all-reduce(f32[16]{0:T(128)S(1)} %psum.193), channel_id=1, replica_groups=mesh['blk_0'=4,'blk_1'=2,'blk_2'=4,'grp_0'=4,'grp_1'=2] {'grp_1'}, use_global_device_ids=true, to_apply=%region_48.0 | all-reduce | flops 16 | bytes 128 | tf_op jit(solution)/shard_map/psum | solution.py:49
  623.1 216.0 %while.188 = (s32[]{:T(128)}, bf16[64,1024]{1,0:T(8,128)(2,1)S(1)}, bf16[16,1024]{1,0:T(8,128)(2,1)S(1)}, f32[32,1024]{1,0:T(8,128)S(1)}, f32[32,128]{1,0:T(8,12...) while((s32[]{:T(128)}, bf16[64,1024]{1,0:T(8,128)(2,1)S(1)}, ...), condition=%wide.region_56.0_spmd, body=%wide.region_52.0_spmd.sunk | while | flops 18685444 | bytes 3470420 | solution.py:141
  623.5 11.7 %collective-permute-done.1 = bf16[16,1024]{1,0:T(8,128)(2,1)S(1)} collective-permute-done((bf16[16,1024]{1,0:T(8,128)(2,1)S(1)}, bf16[16,1024]{1,0:T(8,128)(2,1)S(1)}, u32[]{:S(2)}, u32[]{:S(2)}) %collective-permute-start.1) | collective-permute-done | bytes 32800 | tf_op jit(solution)/shard_map/while/body/eval_jaxpr/ppermute | solution.py:34
  639.1 11.0 %collective-permute-done.1 = bf16[16,1024]{1,0:T(8,128)(2,1)S(1)} collective-permute-done((bf16[16,1024]{1,0:T(8,128)(2,1)S(1)}, bf16[16,1024]{1,0:T(8,128)(2,1)S(1)}, u32[]{:S(2)}, u32[]{:S(2)}) %collective-permute-start.1) | collective-permute-done | bytes 32800 | tf_op jit(solution)/shard_map/while/body/eval_jaxpr/ppermute | solution.py:34
  654.0 10.1 %collective-permute-done.1 = bf16[16,1024]{1,0:T(8,128)(2,1)S(1)} collective-permute-done((bf16[16,1024]{1,0:T(8,128)(2,1)S(1)}, bf16[16,1024]{1,0:T(8,128)(2,1)S(1)}, u32[]{:S(2)}, u32[]{:S(2)}) %collective-permute-start.1) | collective-permute-done | bytes 32800 | tf_op jit(solution)/shard_map/while/body/eval_jaxpr/ppermute | solution.py:34
  668.1 9.6 %collective-permute-done.1 = bf16[16,1024]{1,0:T(8,128)(2,1)S(1)} collective-permute-done((bf16[16,1024]{1,0:T(8,128)(2,1)S(1)}, bf16[16,1024]{1,0:T(8,128)(2,1)S(1)}, u32[]{:S(2)}, u32[]{:S(2)}) %collective-permute-start.1) | collective-permute-done | bytes 32800 | tf_op jit(solution)/shard_map/while/body/eval_jaxpr/ppermute | solution.py:34
  681.6 9.6 %collective-permute-done.1 = bf16[16,1024]{1,0:T(8,128)(2,1)S(1)} collective-permute-done((bf16[16,1024]{1,0:T(8,128)(2,1)S(1)}, bf16[16,1024]{1,0:T(8,128)(2,1)S(1)}, u32[]{:S(2)}, u32[]{:S(2)}) %collective-permute-start.1) | collective-permute-done | bytes 32800 | tf_op jit(solution)/shard_map/while/body/eval_jaxpr/ppermute | solution.py:34
  695.1 9.6 %collective-permute-done.1 = bf16[16,1024]{1,0:T(8,128)(2,1)S(1)} collective-permute-done((bf16[16,1024]{1,0:T(8,128)(2,1)S(1)}, bf16[16,1024]{1,0:T(8,128)(2,1)S(1)}, u32[]{:S(2)}, u32[]{:S(2)}) %collective-permute-start.1) | collective-permute-done | bytes 32800 | tf_op jit(solution)/shard_map/while/body/eval_jaxpr/ppermute | solution.py:34
  708.6 9.6 %collective-permute-done.1 = bf16[16,1024]{1,0:T(8,128)(2,1)S(1)} collective-permute-done((bf16[16,1024]{1,0:T(8,128)(2,1)S(1)}, bf16[16,1024]{1,0:T(8,128)(2,1)S(1)}, u32[]{:S(2)}, u32[]{:S(2)}) %collective-permute-start.1) | collective-permute-done | bytes 32800 | tf_op jit(solution)/shard_map/while/body/eval_jaxpr/ppermute | solution.py:34
  722.1 9.6 %collective-permute-done.1 = bf16[16,1024]{1,0:T(8,128)(2,1)S(1)} collective-permute-done((bf16[16,1024]{1,0:T(8,128)(2,1)S(1)}, bf16[16,1024]{1,0:T(8,128)(2,1)S(1)}, u32[]{:S(2)}, u32[]{:S(2)}) %collective-permute-start.1) | collective-permute-done | bytes 32800 | tf_op jit(solution)/shard_map/while/body/eval_jaxpr/ppermute | solution.py:34
  735.6 9.6 %collective-permute-done.1 = bf16[16,1024]{1,0:T(8,128)(2,1)S(1)} collective-permute-done((bf16[16,1024]{1,0:T(8,128)(2,1)S(1)}, bf16[16,1024]{1,0:T(8,128)(2,1)S(1)}, u32[]{:S(2)}, u32[]{:S(2)}) %collective-permute-start.1) | collective-permute-done | bytes 32800 | tf_op jit(solution)/shard_map/while/body/eval_jaxpr/ppermute | solution.py:34
  762.6 9.9 %collective-permute-done.1 = bf16[16,1024]{1,0:T(8,128)(2,1)S(1)} collective-permute-done((bf16[16,1024]{1,0:T(8,128)(2,1)S(1)}, bf16[16,1024]{1,0:T(8,128)(2,1)S(1)}, u32[]{:S(2)}, u32[]{:S(2)}) %collective-permute-start.1) | collective-permute-done | bytes 32800 | tf_op jit(solution)/shard_map/while/body/eval_jaxpr/ppermute | solution.py:34
  776.4 11.1 %collective-permute-done.1 = bf16[16,1024]{1,0:T(8,128)(2,1)S(1)} collective-permute-done((bf16[16,1024]{1,0:T(8,128)(2,1)S(1)}, bf16[16,1024]{1,0:T(8,128)(2,1)S(1)}, u32[]{:S(2)}, u32[]{:S(2)}) %collective-permute-start.1) | collective-permute-done | bytes 32800 | tf_op jit(solution)/shard_map/while/body/eval_jaxpr/ppermute | solution.py:34
  791.4 12.2 %collective-permute-done.1 = bf16[16,1024]{1,0:T(8,128)(2,1)S(1)} collective-permute-done((bf16[16,1024]{1,0:T(8,128)(2,1)S(1)}, bf16[16,1024]{1,0:T(8,128)(2,1)S(1)}, u32[]{:S(2)}, u32[]{:S(2)}) %collective-permute-start.1) | collective-permute-done | bytes 32800 | tf_op jit(solution)/shard_map/while/body/eval_jaxpr/ppermute | solution.py:34
  807.5 12.5 %collective-permute-done.1 = bf16[16,1024]{1,0:T(8,128)(2,1)S(1)} collective-permute-done((bf16[16,1024]{1,0:T(8,128)(2,1)S(1)}, bf16[16,1024]{1,0:T(8,128)(2,1)S(1)}, u32[]{:S(2)}, u32[]{:S(2)}) %collective-permute-start.1) | collective-permute-done | bytes 32800 | tf_op jit(solution)/shard_map/while/body/eval_jaxpr/ppermute | solution.py:34
  823.8 11.6 %collective-permute-done.1 = bf16[16,1024]{1,0:T(8,128)(2,1)S(1)} collective-permute-done((bf16[16,1024]{1,0:T(8,128)(2,1)S(1)}, bf16[16,1024]{1,0:T(8,128)(2,1)S(1)}, u32[]{:S(2)}, u32[]{:S(2)}) %collective-permute-start.1) | collective-permute-done | bytes 32800 | tf_op jit(solution)/shard_map/while/body/eval_jaxpr/ppermute | solution.py:34
  846.8 20.9 %all-to-all-start.6 = ((f32[8,32,128]{2,1,0:T(8,128)}), f32[8,32,128]{2,1,0:T(8,128)S(1)}, u32[]{:S(2)}, u32[]{:S(2)}) async-start(f32[8,32,128]{2,1,0:T(8,128)} %copy.14), calls=%async_computation.6 | async-start | bytes 262144 | tf_op jit(solution)/shard_map/all_to_all | solution.py:44
  901.6 9.6 %psum.199 = f32[3]{0:T(128)S(1)} all-reduce(f32[3]{0:T(128)S(1)} %psum.198), channel_id=1, replica_groups=mesh['blk_0'=4,'blk_1'=2,'blk_2'=4,'grp_0'=4,'grp_1'=2] {'grp_1'}, use_global_device_ids=true, to_apply=%region_68.69 | all-reduce | flops 3 | bytes 24 | tf_op jit(solution)/shard_map/psum | solution.py:49
  (1042 shorter events, 711.0 us)
Async XLA Ops:
  19.1 12.2 %all-to-all-start = ((bf16[8,64,128]{2,1,0:T(8,128)(2,1)}), bf16[8,64,128]{2,1,0:T(8,128)(2,1)S(1)}, u32[]{:S(2)}, u32[]{:S(2)}) async-start(bf16[8,64,128]{2,1,0:T(8,128)(2,1)} %broadcast_in_dim.86), calls=%async_computation | async-start | bytes 262144 | tf_op jit(solution)/shard_map/all_to_all | solution.py:18
  156.1 11.8 %collective-permute-start.6 = (bf16[64,1024]{1,0:T(8,128)(2,1)S(1)}, bf16[64,1024]{1,0:T(8,128)(2,1)S(1)}, u32[]{:S(2)}, u32[]{:S(2)}) collective-permute-start(bf16[64,1024]{1,0:T(8,128)(2,1)S(1)} %get-tuple-element.2681), channel_id=1, source_target_pairs={{0,8},{8,16},{16,24},{24,32},{32,40},{40,48},{48,56},{56,64},{64,7... | collective-permute-start | bytes 393224 | tf_op jit(solution)/shard_map/while/body/eval_jaxpr/ppermute | solution.py:34
  156.2 11.7 %collective-permute-start.8 = (f32[16,1024]{1,0:T(8,128)S(1)}, f32[16,1024]{1,0:T(8,128)S(1)}, u32[]{:S(2)}, u32[]{:S(2)}) collective-permute-start(f32[16,1024]{1,0:T(8,128)S(1)} %get-tuple-element.2683), channel_id=1, source_target_pairs={{0,8},{8,16},{16,24},{24,32},{32,40},{40,48},{48,56},{56,64},{64,7... | collective-permute-start | bytes 196616 | tf_op jit(solution)/shard_map/while/body/eval_jaxpr/ppermute | solution.py:34
  156.3 11.6 %collective-permute-start.7 = (bf16[16,1024]{1,0:T(8,128)(2,1)S(1)}, bf16[16,1024]{1,0:T(8,128)(2,1)S(1)}, u32[]{:S(2)}, u32[]{:S(2)}) collective-permute-start(bf16[16,1024]{1,0:T(8,128)(2,1)S(1)} %get-tuple-element.2682), channel_id=1, source_target_pairs={{0,8},{8,16},{16,24},{24,32},{32,40},{40,48},{48,56},{56,64},{64,7... | collective-permute-start | bytes 98312 | tf_op jit(solution)/shard_map/while/body/eval_jaxpr/ppermute | solution.py:34
  221.1 29.0 %collective-permute-start.10 = (bf16[64,1024]{1,0:T(8,128)(2,1)S(1)}, bf16[64,1024]{1,0:T(8,128)(2,1)S(1)}, u32[]{:S(2)}, u32[]{:S(2)}) collective-permute-start(bf16[64,1024]{1,0:T(8,128)(2,1)S(1)} %get-tuple-element.1513), channel_id=1, source_target_pairs={{0,8},{8,16},{16,24},{24,32},{32,40},{40,48},{48,56},{56,64},{64,7... | collective-permute-start | bytes 393224 | tf_op jit(solution)/shard_map/ppermute | solution.py:34
  221.2 28.8 %collective-permute-start.9 = (bf16[16,1024]{1,0:T(8,128)(2,1)S(1)}, bf16[16,1024]{1,0:T(8,128)(2,1)S(1)}, u32[]{:S(2)}, u32[]{:S(2)}) collective-permute-start(bf16[16,1024]{1,0:T(8,128)(2,1)S(1)} %get-tuple-element.1512), channel_id=1, source_target_pairs={{0,8},{8,16},{16,24},{24,32},{32,40},{40,48},{48,56},{56,64},{64,7... | collective-permute-start | bytes 98312 | tf_op jit(solution)/shard_map/ppermute | solution.py:34
  228.0 29.5 %all-to-all-start.2 = ((f32[8,16,128]{2,1,0:T(8,128)}), f32[8,16,128]{2,1,0:T(8,128)S(1)}, u32[]{:S(2)}, u32[]{:S(2)}) async-start(f32[8,16,128]{2,1,0:T(8,128)} %copy.10), calls=%async_computation.2 | async-start | bytes 131072 | tf_op jit(solution)/shard_map/all_to_all | solution.py:44
  330.8 12.4 %all-to-all-start.3 = ((bf16[8,16,128]{2,1,0:T(8,128)(2,1)}), bf16[8,16,128]{2,1,0:T(8,128)(2,1)S(1)}, u32[]{:S(2)}, u32[]{:S(2)}) async-start(bf16[8,16,128]{2,1,0:T(8,128)(2,1)} %broadcast_in_dim.88), calls=%async_computation.3 | async-start | bytes 65536 | tf_op jit(solution)/shard_map/all_to_all | solution.py:18
  481.0 11.8 %collective-permute-start.3 = (bf16[64,1024]{1,0:T(8,128)(2,1)S(1)}, bf16[64,1024]{1,0:T(8,128)(2,1)S(1)}, u32[]{:S(2)}, u32[]{:S(2)}) collective-permute-start(bf16[64,1024]{1,0:T(8,128)(2,1)S(1)} %get-tuple-element.2792), channel_id=1, source_target_pairs={{0,8},{8,16},{16,24},{24,32},{32,40},{40,48},{48,56},{56,64},{64,7... | collective-permute-start | bytes 393224 | tf_op jit(solution)/shard_map/while/body/eval_jaxpr/ppermute | solution.py:34
  481.1 11.7 %collective-permute-start.5 = (f32[16,1024]{1,0:T(8,128)S(1)}, f32[16,1024]{1,0:T(8,128)S(1)}, u32[]{:S(2)}, u32[]{:S(2)}) collective-permute-start(f32[16,1024]{1,0:T(8,128)S(1)} %get-tuple-element.2794), channel_id=1, source_target_pairs={{0,8},{8,16},{16,24},{24,32},{32,40},{40,48},{48,56},{56,64},{64,7... | collective-permute-start | bytes 196616 | tf_op jit(solution)/shard_map/while/body/eval_jaxpr/ppermute | solution.py:34
  481.2 11.6 %collective-permute-start.4 = (bf16[16,1024]{1,0:T(8,128)(2,1)S(1)}, bf16[16,1024]{1,0:T(8,128)(2,1)S(1)}, u32[]{:S(2)}, u32[]{:S(2)}) collective-permute-start(bf16[16,1024]{1,0:T(8,128)(2,1)S(1)} %get-tuple-element.2793), channel_id=1, source_target_pairs={{0,8},{8,16},{16,24},{24,32},{32,40},{40,48},{48,56},{56,64},{64,7... | collective-permute-start | bytes 98312 | tf_op jit(solution)/shard_map/while/body/eval_jaxpr/ppermute | solution.py:34
  534.0 28.0 %collective-permute-start.13 = (bf16[64,1024]{1,0:T(8,128)(2,1)S(1)}, bf16[64,1024]{1,0:T(8,128)(2,1)S(1)}, u32[]{:S(2)}, u32[]{:S(2)}) collective-permute-start(bf16[64,1024]{1,0:T(8,128)(2,1)S(1)} %get-tuple-element.1519), channel_id=1, source_target_pairs={{0,8},{8,16},{16,24},{24,32},{32,40},{40,48},{48,56},{56,64},{64,7... | collective-permute-start | bytes 393224 | tf_op jit(solution)/shard_map/ppermute | solution.py:34
  534.4 27.7 %collective-permute-start.12 = (bf16[16,1024]{1,0:T(8,128)(2,1)S(1)}, bf16[16,1024]{1,0:T(8,128)(2,1)S(1)}, u32[]{:S(2)}, u32[]{:S(2)}) collective-permute-start(bf16[16,1024]{1,0:T(8,128)(2,1)S(1)} %get-tuple-element.1518), channel_id=1, source_target_pairs={{0,8},{8,16},{16,24},{24,32},{32,40},{40,48},{48,56},{56,64},{64,7... | collective-permute-start | bytes 98312 | tf_op jit(solution)/shard_map/ppermute | solution.py:34
  541.2 28.4 %all-to-all-start.4 = ((f32[8,16,128]{2,1,0:T(8,128)}), f32[8,16,128]{2,1,0:T(8,128)S(1)}, u32[]{:S(2)}, u32[]{:S(2)}) async-start(f32[8,16,128]{2,1,0:T(8,128)} %copy.12), calls=%async_computation.4 | async-start | bytes 131072 | tf_op jit(solution)/shard_map/all_to_all | solution.py:44
  607.8 12.5 %all-to-all-start.5 = ((bf16[8,16,128]{2,1,0:T(8,128)(2,1)}), bf16[8,16,128]{2,1,0:T(8,128)(2,1)S(1)}, u32[]{:S(2)}, u32[]{:S(2)}) async-start(bf16[8,16,128]{2,1,0:T(8,128)(2,1)} %broadcast_in_dim.91), calls=%async_computation.5 | async-start | bytes 65536 | tf_op jit(solution)/shard_map/all_to_all | solution.py:18
  623.1 12.1 %collective-permute-start.2 = (f32[32,1024]{1,0:T(8,128)S(1)}, f32[32,1024]{1,0:T(8,128)S(1)}, u32[]{:S(2)}, u32[]{:S(2)}) collective-permute-start(f32[32,1024]{1,0:T(8,128)S(1)} %get-tuple-element.2909), channel_id=1, source_target_pairs={{0,8},{8,16},{16,24},{24,32},{32,40},{40,48},{48,56},{56,64},{64,7... | collective-permute-start | bytes 393224 | tf_op jit(solution)/shard_map/while/body/eval_jaxpr/ppermute | solution.py:34
  623.2 12.0 %collective-permute-start = (bf16[64,1024]{1,0:T(8,128)(2,1)S(1)}, bf16[64,1024]{1,0:T(8,128)(2,1)S(1)}, u32[]{:S(2)}, u32[]{:S(2)}) collective-permute-start(bf16[64,1024]{1,0:T(8,128)(2,1)S(1)} %get-tuple-element.2907), channel_id=1, source_target_pairs={{0,8},{8,16},{16,24},{24,32},{32,40},{40,48},{48,56},{56,64},{64,7... | collective-permute-start | bytes 393224 | tf_op jit(solution)/shard_map/while/body/eval_jaxpr/ppermute | solution.py:34
  623.4 11.8 %collective-permute-start.1 = (bf16[16,1024]{1,0:T(8,128)(2,1)S(1)}, bf16[16,1024]{1,0:T(8,128)(2,1)S(1)}, u32[]{:S(2)}, u32[]{:S(2)}) collective-permute-start(bf16[16,1024]{1,0:T(8,128)(2,1)S(1)} %get-tuple-element.2908), channel_id=1, source_target_pairs={{0,8},{8,16},{16,24},{24,32},{32,40},{40,48},{48,56},{56,64},{64,7... | collective-permute-start | bytes 98312 | tf_op jit(solution)/shard_map/while/body/eval_jaxpr/ppermute | solution.py:34
  638.9 11.3 %collective-permute-start.2 = (f32[32,1024]{1,0:T(8,128)S(1)}, f32[32,1024]{1,0:T(8,128)S(1)}, u32[]{:S(2)}, u32[]{:S(2)}) collective-permute-start(f32[32,1024]{1,0:T(8,128)S(1)} %get-tuple-element.2909), channel_id=1, source_target_pairs={{0,8},{8,16},{16,24},{24,32},{32,40},{40,48},{48,56},{56,64},{64,7... | collective-permute-start | bytes 393224 | tf_op jit(solution)/shard_map/while/body/eval_jaxpr/ppermute | solution.py:34
  776.1 11.3 %collective-permute-start.2 = (f32[32,1024]{1,0:T(8,128)S(1)}, f32[32,1024]{1,0:T(8,128)S(1)}, u32[]{:S(2)}, u32[]{:S(2)}) collective-permute-start(f32[32,1024]{1,0:T(8,128)S(1)} %get-tuple-element.2909), channel_id=1, source_target_pairs={{0,8},{8,16},{16,24},{24,32},{32,40},{40,48},{48,56},{56,64},{64,7... | collective-permute-start | bytes 393224 | tf_op jit(solution)/shard_map/while/body/eval_jaxpr/ppermute | solution.py:34
  791.1 12.5 %collective-permute-start.2 = (f32[32,1024]{1,0:T(8,128)S(1)}, f32[32,1024]{1,0:T(8,128)S(1)}, u32[]{:S(2)}, u32[]{:S(2)}) collective-permute-start(f32[32,1024]{1,0:T(8,128)S(1)} %get-tuple-element.2909), channel_id=1, source_target_pairs={{0,8},{8,16},{16,24},{24,32},{32,40},{40,48},{48,56},{56,64},{64,7... | collective-permute-start | bytes 393224 | tf_op jit(solution)/shard_map/while/body/eval_jaxpr/ppermute | solution.py:34
  791.2 12.4 %collective-permute-start = (bf16[64,1024]{1,0:T(8,128)(2,1)S(1)}, bf16[64,1024]{1,0:T(8,128)(2,1)S(1)}, u32[]{:S(2)}, u32[]{:S(2)}) collective-permute-start(bf16[64,1024]{1,0:T(8,128)(2,1)S(1)} %get-tuple-element.2907), channel_id=1, source_target_pairs={{0,8},{8,16},{16,24},{24,32},{32,40},{40,48},{48,56},{56,64},{64,7... | collective-permute-start | bytes 393224 | tf_op jit(solution)/shard_map/while/body/eval_jaxpr/ppermute | solution.py:34
  791.3 12.3 %collective-permute-start.1 = (bf16[16,1024]{1,0:T(8,128)(2,1)S(1)}, bf16[16,1024]{1,0:T(8,128)(2,1)S(1)}, u32[]{:S(2)}, u32[]{:S(2)}) collective-permute-start(bf16[16,1024]{1,0:T(8,128)(2,1)S(1)} %get-tuple-element.2908), channel_id=1, source_target_pairs={{0,8},{8,16},{16,24},{24,32},{32,40},{40,48},{48,56},{56,64},{64,7... | collective-permute-start | bytes 98312 | tf_op jit(solution)/shard_map/while/body/eval_jaxpr/ppermute | solution.py:34
  807.2 12.7 %collective-permute-start.2 = (f32[32,1024]{1,0:T(8,128)S(1)}, f32[32,1024]{1,0:T(8,128)S(1)}, u32[]{:S(2)}, u32[]{:S(2)}) collective-permute-start(f32[32,1024]{1,0:T(8,128)S(1)} %get-tuple-element.2909), channel_id=1, source_target_pairs={{0,8},{8,16},{16,24},{24,32},{32,40},{40,48},{48,56},{56,64},{64,7... | collective-permute-start | bytes 393224 | tf_op jit(solution)/shard_map/while/body/eval_jaxpr/ppermute | solution.py:34
  807.3 12.6 %collective-permute-start = (bf16[64,1024]{1,0:T(8,128)(2,1)S(1)}, bf16[64,1024]{1,0:T(8,128)(2,1)S(1)}, u32[]{:S(2)}, u32[]{:S(2)}) collective-permute-start(bf16[64,1024]{1,0:T(8,128)(2,1)S(1)} %get-tuple-element.2907), channel_id=1, source_target_pairs={{0,8},{8,16},{16,24},{24,32},{32,40},{40,48},{48,56},{56,64},{64,7... | collective-permute-start | bytes 393224 | tf_op jit(solution)/shard_map/while/body/eval_jaxpr/ppermute | solution.py:34
  807.4 12.5 %collective-permute-start.1 = (bf16[16,1024]{1,0:T(8,128)(2,1)S(1)}, bf16[16,1024]{1,0:T(8,128)(2,1)S(1)}, u32[]{:S(2)}, u32[]{:S(2)}) collective-permute-start(bf16[16,1024]{1,0:T(8,128)(2,1)S(1)} %get-tuple-element.2908), channel_id=1, source_target_pairs={{0,8},{8,16},{16,24},{24,32},{32,40},{40,48},{48,56},{56,64},{64,7... | collective-permute-start | bytes 98312 | tf_op jit(solution)/shard_map/while/body/eval_jaxpr/ppermute | solution.py:34
  823.6 11.9 %collective-permute-start.2 = (f32[32,1024]{1,0:T(8,128)S(1)}, f32[32,1024]{1,0:T(8,128)S(1)}, u32[]{:S(2)}, u32[]{:S(2)}) collective-permute-start(f32[32,1024]{1,0:T(8,128)S(1)} %get-tuple-element.2909), channel_id=1, source_target_pairs={{0,8},{8,16},{16,24},{24,32},{32,40},{40,48},{48,56},{56,64},{64,7... | collective-permute-start | bytes 393224 | tf_op jit(solution)/shard_map/while/body/eval_jaxpr/ppermute | solution.py:34
  823.6 11.8 %collective-permute-start = (bf16[64,1024]{1,0:T(8,128)(2,1)S(1)}, bf16[64,1024]{1,0:T(8,128)(2,1)S(1)}, u32[]{:S(2)}, u32[]{:S(2)}) collective-permute-start(bf16[64,1024]{1,0:T(8,128)(2,1)S(1)} %get-tuple-element.2907), channel_id=1, source_target_pairs={{0,8},{8,16},{16,24},{24,32},{32,40},{40,48},{48,56},{56,64},{64,7... | collective-permute-start | bytes 393224 | tf_op jit(solution)/shard_map/while/body/eval_jaxpr/ppermute | solution.py:34
  823.7 11.7 %collective-permute-start.1 = (bf16[16,1024]{1,0:T(8,128)(2,1)S(1)}, bf16[16,1024]{1,0:T(8,128)(2,1)S(1)}, u32[]{:S(2)}, u32[]{:S(2)}) collective-permute-start(bf16[16,1024]{1,0:T(8,128)(2,1)S(1)} %get-tuple-element.2908), channel_id=1, source_target_pairs={{0,8},{8,16},{16,24},{24,32},{32,40},{40,48},{48,56},{56,64},{64,7... | collective-permute-start | bytes 98312 | tf_op jit(solution)/shard_map/while/body/eval_jaxpr/ppermute | solution.py:34
  839.1 28.5 %collective-permute-start.16 = (bf16[64,1024]{1,0:T(8,128)(2,1)S(1)}, bf16[64,1024]{1,0:T(8,128)(2,1)S(1)}, u32[]{:S(2)}, u32[]{:S(2)}) collective-permute-start(bf16[64,1024]{1,0:T(8,128)(2,1)S(1)} %get-tuple-element.1525), channel_id=1, source_target_pairs={{0,8},{8,16},{16,24},{24,32},{32,40},{40,48},{48,56},{56,64},{64,7... | collective-permute-start | bytes 393224 | tf_op jit(solution)/shard_map/ppermute | solution.py:34
  839.2 28.4 %collective-permute-start.15 = (bf16[16,1024]{1,0:T(8,128)(2,1)S(1)}, bf16[16,1024]{1,0:T(8,128)(2,1)S(1)}, u32[]{:S(2)}, u32[]{:S(2)}) collective-permute-start(bf16[16,1024]{1,0:T(8,128)(2,1)S(1)} %get-tuple-element.1524), channel_id=1, source_target_pairs={{0,8},{8,16},{16,24},{24,32},{32,40},{40,48},{48,56},{56,64},{64,7... | collective-permute-start | bytes 98312 | tf_op jit(solution)/shard_map/ppermute | solution.py:34
  846.8 28.9 %all-to-all-start.6 = ((f32[8,32,128]{2,1,0:T(8,128)}), f32[8,32,128]{2,1,0:T(8,128)S(1)}, u32[]{:S(2)}, u32[]{:S(2)}) async-start(f32[8,32,128]{2,1,0:T(8,128)} %copy.14), calls=%async_computation.6 | async-start | bytes 262144 | tf_op jit(solution)/shard_map/all_to_all | solution.py:44
  (121 other events, 1410.8 us)
where the time goes:
time: 914 us; the launch traced here: 912 us
  waiting for transfers between devices  491 us (54%)
  blocking collectives  158 us (17%)
  matrix products  142 us (16%)
  starting transfers between devices  95.9 us (10%)
  other arithmetic  10.2 us (1%)
    ppermute x144, waiting for transfers between devices, shifted(): return lax.ppermute(x, axis, [(i, (i + by) % size) for i in range(size)])  454 us
    psum x20, blocking collectives, one_axis_at_a_time(): return functools.reduce(lax.psum, axes, x)  141 us
    dot_general x94, matrix products, kernel_tiles(): lax.dot_general(own_points, tile_points, (((0,), (0,)), ((), ())), prefer...  95.4 us
    all_to_all x3, starting transfers between devices, summed_on_arrival(): lax.all_to_all(tiles, axis, split_axis=0, concat_axis=0, tiled=True)  63.9 us
    dot_general x136, matrix products, apply_columns(): lax.dot_general(tile_vectors, single, (((1,), (1,)), ((), ())), preferred...  29 us
    all_to_all x3, waiting for transfers between devices, from_everyone(): return lax.all_to_all(copies, axis, split_axis=0, concat_axis=0, tiled=True)  22 us
  transfers between devices with their start and end apart: 150, of which 54 were waited for; matrix products, arithmetic and copies ran while one was open for 1% of the time, Pallas kernels for 0%

commit v1 on v0

v1 whole, which is shorter than its diff:
```python
import math

import jax
import jax.numpy as jnp
from jax import lax
from jax.experimental import pallas as pl
from jax.experimental.pallas import tpu as pltpu
from jax.sharding import Mesh
from jax.sharding import PartitionSpec as P

AXES = ("x", "zl", "y", "zh", "c")
BY_ID = pl.DeviceIdType.MESH
F32 = jnp.float32
BF16 = jnp.bfloat16
DEPTH = 80


def add_all(terms):
    total = terms[0]
    for term in terms[1:]:
        total = total + term
    return total


def make_kernel(sizes, columns, width, total_points):
    xs, zls, ys, zhs, cs = sizes
    zs, gs = zls * zhs, ys * cs
    half = zs // 2
    x_tiles, row_tiles = zs // 2, gs // 2
    tiles = xs * x_tiles
    copies_in_all = 4 * (zs - 1) + 8 * (gs - 1) + 18 + (xs - 1)

    def kernel(
        points,
        right,
        length_ref,
        scale_ref,
        noise_ref,
        solution_out,
        residual_out,
        gradient_out,
        cols,
        r0c,
        a1c,
        rows,
        r0r,
        a1r,
        d2r,
        weights,
        kmat,
        gmat,
        acc,
        vb2,
        rs1,
        rs2,
        ex1,
        ex2,
        fin_g,
        fin_z,
        fin_x,
        send_sems,
        recv_sems,
    ):
        x, y, c = lax.axis_index("x"), lax.axis_index("y"), lax.axis_index("c")
        z = lax.axis_index("zh") * zls + lax.axis_index("zl")

        def z_peer(k):
            to = lax.rem(z + k, zs)
            return {"zl": lax.rem(to, zls), "zh": lax.div(to, zls)}

        def g_peer(dy, dc):
            return {"y": lax.rem(y + dy, ys), "c": lax.rem(c + dc, cs)}

        def x_peer(k):
            return {"x": lax.rem(x + k, xs)}

        started = []

        def send(src, dst, device):
            index = len(started)
            copy = pltpu.make_async_remote_copy(
                src_ref=src,
                dst_ref=dst,
                send_sem=send_sems.at[index],
                recv_sem=recv_sems.at[index],
                device_id=device,
                device_id_type=BY_ID,
            )
            copy.start()
            started.append(copy)
            return copy

        def to_z(src, slots):
            return [send(src, slots(k), z_peer(k)) for k in range(1, zs)]

        def to_g(src, slots):
            return [send(src, slots(s), g_peer(s // cs, s % cs)) for s in range(1, gs)]

        def scatter_g(source, slots):
            return [
                send(source(s), slots(((ys - s // cs) % ys) * cs + s % cs), g_peer(ys - s // cs, s % cs))
                for s in range(1, gs)
            ]

        def wait(copies):
            for copy in copies:
                copy.wait_recv()

        own = points[...].astype(F32)
        norm = jnp.sum(own * own, axis=0, keepdims=True)
        high = norm.astype(BF16).astype(F32)
        middle = (norm - high).astype(BF16).astype(F32)
        low = norm - high - middle
        line = lax.broadcasted_iota(jnp.int32, (DEPTH - 64, width), 0)
        pieces = jnp.where(line % 3 == 0, high, jnp.where(line % 3 == 1, middle, low))
        first, second = line < 3, (line >= 3) & (line < 6)
        cols[0, 0, 0:64, :] = points[...]
        cols[0, 0, 64:DEPTH, :] = jnp.where(first, pieces, jnp.where(second, 1.0, 0.0)).astype(BF16)
        rows[0, 0:64, :] = (own * -2.0).astype(BF16)
        rows[0, 64:DEPTH, :] = jnp.where(first, 1.0, jnp.where(second, pieces, 0.0)).astype(BF16)
        r0c[0, 0] = right[...]
        r0r[0] = right[...]
        acc[0] = jnp.zeros_like(acc[0])
        acc[1] = jnp.zeros_like(acc[1])

        barrier = pltpu.get_barrier_semaphore()
        peers = [z_peer(k) for k in range(1, zs)] + [g_peer(s // cs, s % cs) for s in range(1, gs)]
        peers += [x_peer(k) for k in range(1, xs)]
        for peer in peers:
            pl.semaphore_signal(barrier, inc=1, device_id=peer, device_id_type=BY_ID)
        pl.semaphore_wait(barrier, len(peers))

        z_cols = to_z(cols.at[0, 0], lambda k: cols.at[0, k])
        g_rows = to_g(rows.at[0], lambda s: rows.at[s])
        z_r0 = to_z(r0c.at[0, 0], lambda k: r0c.at[0, k])
        g_r0 = to_g(r0r.at[0], lambda s: r0r.at[s])

        inv = jnp.max(1.0 / jnp.full((8, 128), length_ref[0], F32))
        root = inv * math.sqrt(5.0)
        rate = inv * (-math.sqrt(5.0) / math.log(2.0))
        third = inv * inv * (5.0 / 3.0)
        slope = inv * inv * inv * (5.0 / 3.0)
        amplitude, jitter = scale_ref[0], noise_ref[0]

        def kernel_pair(inner):
            dist = jnp.maximum(inner, 1e-30)
            root_dist = dist * lax.rsqrt(dist)
            damping = jnp.exp2(root_dist * rate)
            linear = root_dist * root + 1.0
            kern = (linear + dist * third) * damping
            dkern = (dist * slope) * linear * damping
            return kern.astype(BF16), dkern.astype(BF16)

        def add_product(which, part, r, product):
            acc[which, part, 2 * r] += product[:, :width]
            acc[which, part, 2 * r + 1] += product[:, width:]

        def sweep(slot, low_tile, high_tile):
            def one_tile(t, carry):
                padding = jnp.zeros((128 - DEPTH, width), F32)
                turned = [
                    jnp.transpose(jnp.concatenate([cols[slot, 2 * t + h].astype(F32), padding], axis=0)).astype(BF16)
                    for h in range(2)
                ]
                turned = jnp.concatenate(turned, axis=0)
                vectors = jnp.concatenate([r0c[slot, 2 * t], r0c[slot, 2 * t + 1]], axis=1).astype(BF16)
                at = slot * x_tiles + t
                for r in range(row_tiles):
                    inner = jnp.dot(turned, weights[r], preferred_element_type=F32)
                    for q in range(0, 2 * width, 32):
                        kern, dkern = kernel_pair(inner[q : q + 32])
                        kmat[at, r, q : q + 32, :] = kern
                        gmat[at, r, q : q + 32, :] = dkern
                    add_product(0, 0, r, jnp.dot(vectors, kmat[at, r], preferred_element_type=F32))
                    add_product(0, 1, r, jnp.dot(vectors, gmat[at, r], preferred_element_type=F32))
                return carry

            lax.fori_loop(low_tile, high_tile, one_tile, 0)

        def start_ring(buffers):
            moves = {}
            for h in range(2):
                part = pl.ds(h * half, half)
                moves["right", h] = [send(b.at[0, part], b.at[1, part], x_peer(1)) for b in buffers]
            for h in (1, 0):
                part = pl.ds(h * half, half)
                moves["left", h] = [send(b.at[0, part], b.at[2, part], x_peer(xs - 1)) for b in buffers]
            return moves

        def pass_on(moves, buffers):
            wait(moves["right", 0])
            moves["far", 0] = [send(b.at[1, pl.ds(0, half)], b.at[3, pl.ds(0, half)], x_peer(1)) for b in buffers]
            wait(moves["left", 1])
            moves["far", 1] = [
                send(b.at[2, pl.ds(half, half)], b.at[3, pl.ds(half, half)], x_peer(xs - 1)) for b in buffers
            ]

        wait(z_cols + z_r0)
        ring = start_ring([cols, r0c])
        wait(g_rows)
        for r in range(row_tiles):
            weights[r, 0:DEPTH, :] = jnp.concatenate([rows[2 * r], rows[2 * r + 1]], axis=1)
            weights[r, DEPTH:128, :] = jnp.zeros((128 - DEPTH, 2 * width), BF16)
        mid = x_tiles // 2
        sweep(0, 0, x_tiles)
        pass_on(ring, [cols, r0c])
        sweep(1, 0, mid)
        sweep(2, mid, x_tiles)
        wait(ring["right", 1])
        sweep(1, mid, x_tiles)
        wait(ring["left", 0])
        sweep(2, 0, mid)
        wait(ring["far", 0])
        sweep(3, 0, mid)
        wait(ring["far", 1])
        sweep(3, mid, x_tiles)

        arriving = scatter_g(lambda s: acc.at[0, 0, s], lambda s: rs1.at[s])
        wait(arriving)
        product = add_all([acc[0, 0, 0]] + [rs1[s] for s in range(1, gs)])
        applied = amplitude * product + jitter * right[...]
        a1c[0, 0] = applied
        a1r[0] = applied
        z_a1 = to_z(a1c.at[0, 0], lambda k: a1c.at[0, k])
        g_a1 = to_g(a1r.at[0], lambda s: a1r.at[s])
        wait(z_a1)
        ring = start_ring([a1c])
        pass_on(ring, [a1c])
        wait(ring["right", 1] + ring["left", 0] + ring["far", 0] + ring["far", 1])

        lane = lax.broadcasted_iota(jnp.int32, (columns, width), 1)

        def pack(sums):
            tile = jnp.zeros((columns, width), F32)
            for index, value in enumerate(sums):
                tile = jnp.where(lane == index, jnp.sum(value, axis=1, keepdims=True), tile)
            return tile

        def take(tile, index):
            return jnp.sum(jnp.where(lane == index, tile, 0.0), axis=1, keepdims=True)

        units = [(i, k) for i in range(xs) for k in range(zs)]
        ex1[0] = pack(
            [add_all([r0c[u] * r0c[u] for u in units]), add_all([r0c[u] * a1c[u] for u in units])]
        )
        wait(to_g(ex1.at[0], lambda s: ex1.at[s]))
        total = add_all([ex1[s] for s in range(gs)])
        rr0, curvature = take(total, 0), take(total, 1)
        step1 = rr0 / curvature

        def new_residual(u):
            return r0c[u] - step1 * a1c[u]

        ex2[0] = pack([add_all([new_residual(u) * new_residual(u) for u in units])])
        wait(to_g(ex2.at[0], lambda s: ex2.at[s]))
        rr1 = take(add_all([ex2[s] for s in range(gs)]), 0)
        ratio = rr1 / rr0
        for i in range(xs):
            for t in range(x_tiles):
                pair = [new_residual((i, 2 * t + h)) + ratio * r0c[i, 2 * t + h] for h in range(2)]
                vb2[i * x_tiles + t] = jnp.concatenate(pair, axis=1).astype(BF16)

        def second_product(part, mat):
            def one_tile(t, carry):
                for r in range(row_tiles):
                    add_product(1, part, r, jnp.dot(vb2[t], mat[t, r], preferred_element_type=F32))
                return carry

            lax.fori_loop(0, tiles, one_tile, 0)

        second_product(0, kmat)
        arriving = scatter_g(lambda s: acc.at[1, 0, s], lambda s: rs2.at[s])
        second_product(1, gmat)

        wait(g_a1 + g_r0)
        for s in range(gs):
            d2r[s] = (r0r[s] - step1 * a1r[s]) + ratio * r0r[s]
        sums = []
        for left in (r0r, d2r):
            for which in range(2):
                for part in range(2):
                    sums.append(add_all([left[s] * acc[which, part, s] for s in range(gs)]))
        sums += [r0r[0] * d2r[0], d2r[0] * d2r[0]]
        fin_g[0] = pack(sums)
        wait(to_g(fin_g.at[0], lambda s: fin_g.at[s]))
        fin_z[0] = add_all([fin_g[s] for s in range(gs)])
        wait(to_z(fin_z.at[0], lambda k: fin_z.at[k]))
        fin_x[0] = add_all([fin_z[k] for k in range(zs)])
        wait([send(fin_x.at[0], fin_x.at[k], x_peer(k)) for k in range(1, xs)])
        total = add_all([fin_x[k] for k in range(xs)])
        (r0_k1, r0_g1, r0_k2, r0_g2, d2_k1, d2_g1, d2_k2, d2_g2, r0_d2, d2_d2) = [take(total, i) for i in range(10)]

        step2 = rr1 / (amplitude * d2_k2 + jitter * d2_d2)
        wait(arriving)
        product = add_all([acc[1, 0, 0]] + [rs2[s] for s in range(1, gs)])
        applied = amplitude * product + jitter * d2r[0]
        solution_out[...] = step1 * right[...] + step2 * d2r[0]
        residual_out[...] = (right[...] - step1 * a1r[0]) - step2 * applied

        top = lax.broadcasted_iota(jnp.int32, (columns, 1), 0) == 0
        weight = jnp.where(top, 1.0, -1.0 / (columns - 1))

        def quadratic(r0_r0, r0_d2, d2_r0, d2_d2):
            plain = step1 * r0_r0 + step2 * r0_d2
            other = step1 * d2_r0 + step2 * d2_d2
            return jnp.sum(weight * jnp.where(top, step1 * plain + step2 * other, plain))

        share = 0.5 / total_points
        gradient_out[0] = quadratic(r0_g1, r0_g2, d2_g1, d2_g2) * amplitude * share
        gradient_out[1] = quadratic(r0_k1, r0_k2, d2_k1, d2_k2) * share
        gradient_out[2] = quadratic(rr0, r0_d2, r0_d2, d2_d2) * share

        assert len(started) == copies_in_all
        for copy in started:
            copy.wait_send()

    unit = (columns, width)
    scratch = [
        pltpu.VMEM((xs, zs, DEPTH, width), BF16),
        pltpu.VMEM((xs, zs, *unit), F32),
        pltpu.VMEM((xs, zs, *unit), F32),
        pltpu.VMEM((gs, DEPTH, width), BF16),
        pltpu.VMEM((gs, *unit), F32),
        pltpu.VMEM((gs, *unit), F32),
        pltpu.VMEM((gs, *unit), F32),
        pltpu.VMEM((row_tiles, 128, 2 * width), BF16),
        pltpu.VMEM((tiles, row_tiles, 2 * width, 2 * width), BF16),
        pltpu.VMEM((tiles, row_tiles, 2 * width, 2 * width), BF16),
        pltpu.VMEM((2, 2, gs, *unit), F32),
        pltpu.VMEM((tiles, columns, 2 * width), BF16),
        pltpu.VMEM((gs, *unit), F32),
        pltpu.VMEM((gs, *unit), F32),
        pltpu.VMEM((gs, *unit), F32),
        pltpu.VMEM((gs, *unit), F32),
        pltpu.VMEM((gs, *unit), F32),
        pltpu.VMEM((zs, *unit), F32),
        pltpu.VMEM((xs, *unit), F32),
        pltpu.SemaphoreType.DMA((copies_in_all,)),
        pltpu.SemaphoreType.DMA((copies_in_all,)),
    ]
    vmem = pl.BlockSpec(memory_space=pltpu.VMEM)
    smem = pl.BlockSpec(memory_space=pltpu.SMEM)
    return pl.pallas_call(
        kernel,
        out_shape=(
            jax.ShapeDtypeStruct(unit, F32),
            jax.ShapeDtypeStruct(unit, F32),
            jax.ShapeDtypeStruct((3,), F32),
        ),
        in_specs=[vmem, vmem, smem, smem, smem],
        out_specs=(vmem, vmem, smem),
        scratch_shapes=scratch,
        compiler_params=pltpu.CompilerParams(
            collective_id=0, has_side_effects=True, vmem_limit_bytes=48 * 1024 * 1024
        ),
    )


def solution(mesh):
    sizes = (4, 2, 4, 4, 2)
    split = Mesh(mesh.devices.reshape(sizes), AXES)

    def local(points, right_side, lengthscale, outputscale, noise_level):
        columns, width = right_side.shape
        call = make_kernel(sizes, columns, width, width * math.prod(sizes))
        return call(points, right_side, lengthscale, outputscale, noise_level)

    return jax.shard_map(
        local,
        mesh=split,
        in_specs=(P(None, AXES), P(None, AXES), P(), P(), P()),
        out_specs=(P(None, AXES), P(None, AXES), P()),
        check_vma=False,
    )
```

time: 914 us -> 81.7 us (0.09)
  waiting for transfers between devices: 491 us -> 0 us
  blocking collectives: 158 us -> 0 us
  matrix products: 142 us -> 0 us
  starting transfers between devices: 95.9 us -> 0 us
  Pallas kernels: 0 us -> 75.7 us
  other arithmetic: 10.2 us -> 0 us
    ppermute x144 -> x0, waiting for transfers between devices: 454 us -> none  [shifted(): return lax.ppermute(x, axis, [(i, (i + by) % size) for i in range(size)])]
    dot_general x350 -> x0, matrix products: 142 us -> none  [the longest x94 95.4 us: kernel_tiles(): lax.dot_general(own_points, tile_points, (((0,), (0,)), ((), ())), prefer...]
    psum x20 -> x0, blocking collectives: 141 us -> none  [one_axis_at_a_time(): return functools.reduce(lax.psum, axes, x)]
    all_to_all x6 -> x0, starting transfers between devices: 78.3 us -> none  [the longest x3 63.9 us: summed_on_arrival(): lax.all_to_all(tiles, axis, split_axis=0, concat_axis=0, tiled=True)]
    pallas_call x0 -> x1, Pallas kernels: none -> 75.7 us  [local(): return call(points, right_side, lengthscale, outputscale, noise_level)]
    all_to_all x6 -> x0, waiting for transfers between devices: 37.3 us -> none  [the longest x3 22 us: from_everyone(): return lax.all_to_all(copies, axis, split_axis=0, concat_axis=0, tiled=True)]
    ppermute x144 -> x0, starting transfers between devices: 17.6 us -> none  [shifted(): return lax.ppermute(x, axis, [(i, (i + by) % size) for i in range(size)])]
    all_to_all x1 -> x0, blocking collectives: 17.1 us -> none  [from_everyone(): return lax.all_to_all(copies, axis, split_axis=0, concat_axis=0, tiled=True)]
  transfers between devices with their start and end apart: 150 -> 0, of which waited for: 54 -> 0; matrix products, arithmetic and copies ran while one was open for 1% -> 0% of each run, Pallas kernels for 0% -> 0%
where the time goes in v1:
time: 81.7 us; the launch traced here: 81.4 us
  Pallas kernels  75.7 us (93%)
  local copies, waits for them, and re-layouts  3.12 us (4%)
  between operations  2.59 us (3%)
    pallas_call x1, Pallas kernels, local(): return call(points, right_side, lengthscale, outputscale, noise_level)  75.7 us
    unnamed x7, local copies, waits for them, and re-layouts  3.12 us

profile of v1, /device:TPU:1, one launch (start us, length us, event | category | flops | bytes accessed | tf_op | source)
XLA Modules:
  0.0 81.4 jit_solution(14440804210232123883)
XLA Ops:
  2.6 0.0 copy-start
  2.6 0.7 copy-done
  3.3 0.0 copy-start.1
  3.3 0.7 copy-done.1
  4.0 75.7 %shard_map.76 = (f32[16,128]{1,0:T(8,128)S(1)}, f32[16,128]{1,0:T(8,128)S(1)}, f32[3]{0:T(128)S(1)}) custom-call(bf16[64,128]{1,0:T(8,128)(2,1)S(1)} %copy-done, f32[16,128]{1,0:T(8,128)S(1)} %copy-done.1, f32[1]{0:T(128)S(6)} %copy.11.length_ref, f32[1]{0:T(128)S(6)} %copy.12.scale_ref, f32[1]{0:T(128)S(6)} %copy.13.noise_ref), custom_call_target="tpu_custom_call" | custom-call | tf_op jit(solution)/shard_map/pallas_call | solution.py:366
  79.7 0.6 copy.14
  80.3 0.6 copy.15
  80.9 0.5 copy.16
Async XLA Ops:
  2.6 0.7 copy-start
  3.3 0.7 copy-start.1

commit v2 on v1

v2 whole, which is shorter than its diff:
```python
import math

import jax
import jax.numpy as jnp
from jax import lax
from jax.experimental import pallas as pl
from jax.experimental.pallas import tpu as pltpu
from jax.sharding import Mesh
from jax.sharding import PartitionSpec as P

AXES = ("x", "zl", "y", "zh", "c")
BY_ID = pl.DeviceIdType.MESH
F32 = jnp.float32
BF16 = jnp.bfloat16
FEATURES = 64
UNIT = 80


def add_all(terms):
    total = terms[0]
    for term in terms[1:]:
        total = total + term
    return total


def two_sum(a, b):
    s = a + b
    t = s - a
    return s, (a - (s - t)) + (b - t)


def pair_sum(a, b):
    s, e = two_sum(a[0], b[0])
    e = e + (a[1] + b[1])
    high = s + e
    return high, e - (high - s)


def halves(a):
    t = a * 4097.0
    high = t - (t - a)
    return high, a - high


def two_product(a, b):
    p = a * b
    (ah, al), (bh, bl) = halves(a), halves(b)
    return p, ((ah * bh - p) + ah * bl + al * bh) + al * bl


def pair_tree(pairs):
    while len(pairs) > 1:
        pairs = [pair_sum(pairs[i], pairs[i + 1]) for i in range(0, len(pairs), 2)]
    return pairs[0]


def make_kernel(sizes, columns, width, total_points):
    xs, zls, ys, zhs, cs = sizes
    zs, gs = zls * zhs, ys * cs
    planes = xs * gs
    half = zs // 2
    x_tiles, row_tiles = zs // 2, gs // 2
    tiles = xs * x_tiles
    wide = 2 * width
    copies_in_all = 3 * (zs - 1) + 5 * (gs - 1) + 18 + 2 * (planes - 1 + zs - 1)
    z_offsets = [0] + [k for d in range(1, half) for k in (d, zs - d)] + [half]

    def kernel(
        points_in,
        right_in,
        length_in,
        scale_in,
        noise_in,
        solution_out,
        residual_out,
        gradient_out,
        cols,
        r0c,
        a1c,
        rows,
        r0r,
        a1r,
        d2r,
        weights,
        kmat,
        gmat,
        acc,
        vb2,
        upright,
        rs1,
        rs2,
        plane1,
        line1,
        plane2,
        line2,
        local_sems,
        send_sems,
        recv_sems,
    ):
        x, y, c = lax.axis_index("x"), lax.axis_index("y"), lax.axis_index("c")
        z = lax.axis_index("zh") * zls + lax.axis_index("zl")

        def z_peer(k):
            to = lax.rem(z + k, zs)
            return {"zl": lax.rem(to, zls), "zh": lax.div(to, zls)}

        def plane_peer(s):
            dx, dy, dc = s // gs, s % gs // cs, s % cs
            return {"x": lax.rem(x + dx, xs), "y": lax.rem(y + dy, ys), "c": lax.rem(c + dc, cs)}

        def x_peer(k):
            return {"x": lax.rem(x + k, xs)}

        barrier = pltpu.get_barrier_semaphore()
        peers = [z_peer(k) for k in range(1, zs)] + [plane_peer(s) for s in range(1, planes)]
        for peer in peers:
            pl.semaphore_signal(barrier, inc=1, device_id=peer, device_id_type=BY_ID)

        fetches = [
            pltpu.make_async_copy(src, dst, local_sems.at[i])
            for i, (src, dst) in enumerate(
                [
                    (right_in, r0c.at[0, 0]),
                    (right_in, r0r.at[0]),
                    (points_in, cols.at[0, 0, pl.ds(0, FEATURES)]),
                    (points_in, rows.at[0]),
                ]
            )
        ]
        for fetch in fetches:
            fetch.start()
        started = []

        def send(src, dst, device):
            index = len(started)
            copy = pltpu.make_async_remote_copy(
                src_ref=src,
                dst_ref=dst,
                send_sem=send_sems.at[index],
                recv_sem=recv_sems.at[index],
                device_id=device,
                device_id_type=BY_ID,
            )
            copy.start()
            started.append(copy)
            return copy

        def to_z(src, slots):
            return [send(src, slots(j), z_peer(z_offsets[j])) for j in range(1, zs)]

        def to_g(src, slots):
            return [send(src, slots(s), plane_peer(s)) for s in range(1, gs)]

        def opposite(s):
            return ((ys - s // cs) % ys) * cs + s % cs

        def wait(copies):
            for copy in copies:
                copy.wait_recv()

        acc[...] = jnp.zeros_like(acc)
        for r in range(row_tiles):
            weights[r, UNIT:128, :] = jnp.zeros((128 - UNIT, wide), BF16)
        for fetch in fetches:
            fetch.wait()
        r0 = r0c[0, 0]
        cols[0, 0, FEATURES:UNIT, :] = r0.astype(BF16)
        pl.semaphore_wait(barrier, len(peers))

        z_cols = to_z(cols.at[0, 0], lambda j: cols.at[0, j])
        g_rows = to_g(rows.at[0], lambda s: rows.at[s])
        inv = jnp.max(1.0 / jnp.full((8, 128), length_in[0], F32))
        root = inv * math.sqrt(5.0)
        rate = inv * (-math.sqrt(5.0) / math.log(2.0))
        third = inv * inv * (5.0 / 3.0)
        amplitude, jitter = scale_in[0], noise_in[0]

        line = lax.broadcasted_iota(jnp.int32, (16, width), 0)
        first, second = line < 3, (line >= 3) & (line < 6)

        def norm_pieces(values):
            norm = jnp.sum(values * values, axis=0, keepdims=True)
            high = norm.astype(BF16).astype(F32)
            middle = (norm - high).astype(BF16).astype(F32)
            low = norm - high - middle
            return jnp.where(line % 3 == 0, high, jnp.where(line % 3 == 1, middle, low))

        def column_side(unit):
            values = unit.astype(F32)
            extra = jnp.where(first, norm_pieces(values), jnp.where(second, 1.0, 0.0))
            padding = jnp.zeros((128 - UNIT, width), F32)
            return jnp.transpose(jnp.concatenate([values, extra, padding], axis=0)).astype(BF16)

        def row_side(unit):
            values = unit.astype(F32)
            extra = jnp.where(first, 1.0, jnp.where(second, norm_pieces(values), 0.0))
            return jnp.concatenate([values * -2.0, extra], axis=0).astype(BF16)

        def kernel_pair(inner):
            dist = jnp.maximum(inner, 1e-30)
            root_dist = dist * lax.rsqrt(dist)
            damping = jnp.exp2(root_dist * rate)
            linear = root_dist * root + 1.0
            bend = dist * third
            plain = linear * damping
            return (plain + bend * damping).astype(BF16), (bend * plain).astype(BF16)

        def add_product(part, r, product):
            acc[part, 2 * r] += product[:, :width]
            acc[part, 2 * r + 1] += product[:, width:]

        def load_tile(slot, t):
            turned = [column_side(cols[slot, 2 * t + h, 0:FEATURES, :]) for h in range(2)]
            vectors = [cols[slot, 2 * t + h, FEATURES:UNIT, :] for h in range(2)]
            return jnp.concatenate(turned, axis=0), jnp.concatenate(vectors, axis=1)

        def one_block(at, r, turned, vectors):
            inner = jnp.dot(turned, weights[r], preferred_element_type=F32)
            for q in range(0, wide, 32):
                kern, dkern = kernel_pair(inner[q : q + 32])
                kmat[r, at, q : q + 32, :] = kern
                gmat[r, at, q : q + 32, :] = dkern
            add_product(0, r, jnp.dot(vectors, kmat[r, at], preferred_element_type=F32))
            add_product(1, r, jnp.dot(vectors, gmat[r, at], preferred_element_type=F32))

        def sweep(slot, low_tile, high_tile):
            def one_tile(t, carry):
                turned, vectors = load_tile(slot, t)
                for r in range(row_tiles):
                    one_block(slot * x_tiles + t, r, turned, vectors)
                return carry

            lax.fori_loop(low_tile, high_tile, one_tile, 0)

        def ring_send(buf, h, slot, way):
            part = pl.ds(h * half, half)
            return [send(buf.at[0, part], buf.at[slot, part], x_peer(way))]

        def ring_rest(buf, ring):
            ring["right", 1] = ring_send(buf, 1, 1, 1)
            ring["left", 1] = ring_send(buf, 1, 2, xs - 1)
            ring["left", 0] = ring_send(buf, 0, 2, xs - 1)

        def pass_right(buf, ring):
            wait(ring["right", 0])
            part = pl.ds(0, half)
            ring["far", 0] = [send(buf.at[1, part], buf.at[3, part], x_peer(1))]

        def pass_left(buf, ring):
            wait(ring["left", 1])
            part = pl.ds(half, half)
            ring["far", 1] = [send(buf.at[2, part], buf.at[3, part], x_peer(xs - 1))]

        mid = x_tiles // 2
        wait(g_rows)
        for r in range(row_tiles):
            weights[r, 0:UNIT, :] = jnp.concatenate([row_side(rows[2 * r]), row_side(rows[2 * r + 1])], axis=1)
        ring = {}
        wait(z_cols[: half - 1])
        ring["right", 0] = ring_send(cols, 0, 1, 1)
        sweep(0, 0, mid)
        wait(z_cols[half - 1 :])
        ring_rest(cols, ring)
        z_r0 = to_z(r0c.at[0, 0], lambda j: r0c.at[0, j])
        g_r0 = to_g(r0r.at[0], lambda s: r0r.at[s])
        sweep(0, mid, x_tiles)
        pass_right(cols, ring)
        sweep(1, 0, mid)
        pass_left(cols, ring)
        sweep(2, mid, x_tiles)
        wait(ring["right", 1])
        sweep(1, mid, x_tiles)
        wait(z_r0)
        ring0 = {("right", 0): ring_send(r0c, 0, 1, 1)}
        ring_rest(r0c, ring0)
        wait(ring["left", 0])
        sweep(2, 0, mid)
        wait(ring["far", 0])
        sweep(3, 0, mid)
        pass_right(r0c, ring0)
        pass_left(r0c, ring0)
        wait(ring["far", 1])

        order = [r for r in range(1, row_tiles)] + [0]
        loaded = [load_tile(3, t) for t in range(mid, x_tiles)]
        arriving = []
        for r in order:
            for t in range(mid, x_tiles):
                one_block(3 * x_tiles + t, r, *loaded[t - mid])
            for s in (2 * r, 2 * r + 1):
                if s:
                    arriving.append(send(acc.at[0, s], rs1.at[opposite(s)], plane_peer(opposite(s))))
        wait(arriving)
        product = add_all([acc[0, 0]] + [rs1[s] for s in range(1, gs)])
        a1 = amplitude * product + jitter * r0
        a1c[0, 0] = a1
        a1r[0] = a1
        z_a1 = to_z(a1c.at[0, 0], lambda j: a1c.at[0, j])
        g_a1 = to_g(a1r.at[0], lambda s: a1r.at[s])

        lane = lax.broadcasted_iota(jnp.int32, (8, 128), 1)

        def stack(parts):
            parts = list(parts) + [jnp.zeros((128 - columns * len(parts), width), F32)] * (columns * len(parts) < 128)
            return jnp.transpose(jnp.concatenate(parts, axis=0))

        def unstack(row):
            turned = jnp.transpose(jnp.broadcast_to(row[0:1], (128, 128)))
            return [turned[columns * i : columns * (i + 1)] for i in range(128 // columns)]

        def sublane_pair(pair):
            for shift in (4, 2, 1):
                pair = pair_sum(pair, tuple(pltpu.roll(v, shift, 0) for v in pair))
            return pair

        def join(pair):
            return jnp.where(lane < 64, pair[0], pltpu.roll(pair[1], 64, 1))

        def split(row):
            return row, pltpu.roll(row, 64, 1)

        def eights(buf, count):
            return [jnp.concatenate([buf[i + j] for j in range(8)], axis=0) for i in range(0, count, 8)]

        def pair_total(buf, count):
            return sublane_pair(pair_tree([split(rows8) for rows8 in eights(buf, count)]))

        products = [two_product(r0, r0), two_product(r0, a1), two_product(a1, a1)]
        high, low = stack([p for p, _ in products]), stack([e for _, e in products])
        own_sums = sublane_pair(pair_tree([(high[i : i + 8], low[i : i + 8]) for i in range(0, 128, 8)]))
        plane1[0] = join(own_sums)[0:1]
        in_plane = [send(plane1.at[0], plane1.at[s], plane_peer(s)) for s in range(1, planes)]

        ring = {}
        wait(z_a1[: half - 1])
        ring["right", 0] = ring_send(a1c, 0, 1, 1)
        wait(z_a1[half - 1 :])
        ring_rest(a1c, ring)
        wait(in_plane)
        line1[0] = join(pair_total(plane1, planes))[0:1]
        in_line = [send(line1.at[0], line1.at[k], z_peer(k)) for k in range(1, zs)]
        pass_right(a1c, ring)
        pass_left(a1c, ring)
        wait(g_a1 + g_r0)
        wait(ring0["right", 1] + ring0["left", 0] + ring0["far", 0] + ring0["far", 1])
        wait(in_line)
        sums = pair_total(line1, zs)

        def aligned(i):
            return tuple(pltpu.roll(v, (128 - columns * i) % 128, 1) if i else v for v in sums)

        rr0_pair, curve_pair, aa_pair = aligned(0), aligned(1), aligned(2)
        step1_row = rr0_pair[0] / curve_pair[0]
        cross, cross_low = two_product(curve_pair[0], -2.0 * step1_row)
        cross = (cross, cross_low - 2.0 * step1_row * curve_pair[1])
        square, square_low = two_product(step1_row, step1_row)
        bend, bend_low = two_product(aa_pair[0], square)
        bend = (bend, bend_low + (aa_pair[0] * square_low + aa_pair[1] * square))
        rr1_pair = pair_sum(pair_sum(rr0_pair, cross), bend)
        rr1_row = rr1_pair[0] + rr1_pair[1]
        packed = step1_row
        for i, row in enumerate((rr1_row / rr0_pair[0], rr1_row, rr0_pair[0])):
            packed = jnp.where(lane >= columns * (i + 1), pltpu.roll(row, columns * (i + 1), 1), packed)
        step1, ratio, rr1, rr0 = unstack(packed)[:4]
        wait(ring["right", 1] + ring["left", 0] + ring["far", 0] + ring["far", 1])

        def new_direction(r0_part, a1_part):
            return (r0_part - step1 * a1_part) + ratio * r0_part

        for i in range(xs):
            for t in range(x_tiles):
                pair = [new_direction(r0c[i, 2 * t + h], a1c[i, 2 * t + h]) for h in range(2)]
                at = i * x_tiles + t
                side, place = at // (tiles // 2), at % (tiles // 2) * wide
                vb2[side, :, place : place + wide] = jnp.concatenate(pair, axis=1).astype(BF16)
                for h in range(2):
                    upright[i * x_tiles + t, h * width : (h + 1) * width, :] = jnp.transpose(
                        jnp.broadcast_to(pair[h][0:1], (width, width))
                    )
        for s in range(gs):
            d2r[s] = new_direction(r0r[s], a1r[s])
        d2 = d2r[0]

        arriving = []
        bilinear = jnp.zeros((16, width), F32)
        for r in order:
            sides = []
            slopes = jnp.zeros((16, wide), F32)
            for side in range(2):
                part = kmat[r, side * (tiles // 2) : (side + 1) * (tiles // 2)].reshape(tiles // 2 * wide, wide)
                sides.append(jnp.dot(vb2[side], part, preferred_element_type=F32))
            for t in range(tiles):
                for q in range(0, wide, 64):
                    scale = upright[t, q : q + 64, :]
                    terms = gmat[r, t, q : q + 64, :].astype(F32) * jnp.concatenate([scale, scale], axis=1)
                    slopes = slopes + add_all([terms[i : i + 16] for i in range(0, 64, 16)])
            total = sides[0] + sides[1]
            for h in range(2):
                s = 2 * r + h
                acc[2, s] = total[:, h * width : (h + 1) * width]
                bilinear = bilinear + slopes[:, h * width : (h + 1) * width] * d2r[s][0:1]
                if s:
                    arriving.append(send(acc.at[2, s], rs2.at[opposite(s)], plane_peer(opposite(s))))

        def dot_rows(left, part):
            return add_all([left[s] * acc[part, s] for s in range(gs)])

        top = lax.broadcasted_iota(jnp.int32, (columns, width), 0) == 0
        slope_rows = jnp.where(top, jnp.sum(bilinear, axis=0, keepdims=True), 0.0)
        stats = [dot_rows(r0r, 0), dot_rows(r0r, 1), dot_rows(d2r, 1), slope_rows]
        stats += [dot_rows(r0r, 2), dot_rows(d2r, 2), r0 * d2, d2 * d2]
        plane2[0] = jnp.sum(stack(stats), axis=0, keepdims=True)
        wait([send(plane2.at[0], plane2.at[s], plane_peer(s)) for s in range(1, planes)])
        line2[0] = jnp.sum(add_all(eights(plane2, planes)), axis=0, keepdims=True)
        wait([send(line2.at[0], line2.at[k], z_peer(k)) for k in range(1, zs)])
        total = jnp.sum(add_all(eights(line2, zs)), axis=0, keepdims=True)
        r0_k1, r0_g1, d2_g1, d2_g2, r0_k2, d2_k2, r0_d2, d2_d2 = unstack(total)

        step2 = rr1 / (amplitude * d2_k2 + jitter * d2_d2)
        wait(arriving)
        product = add_all([acc[2, 0]] + [rs2[s] for s in range(1, gs)])
        applied = amplitude * product + jitter * d2
        solution_out[...] = step1 * r0 + step2 * d2
        residual_out[...] = (r0 - step1 * a1) - step2 * applied

        weight = jnp.where(top, 1.0, -1.0 / (columns - 1))

        def quadratic(r0_r0, mixed, d2_d2):
            plain = step1 * r0_r0 + step2 * mixed
            other = step1 * mixed + step2 * d2_d2
            terms = weight * jnp.where(top, step1 * plain + step2 * other, plain)
            return jnp.sum(terms[:, 0:1])

        share = 0.5 / total_points
        gradient_out[0] = quadratic(r0_g1, d2_g1, d2_g2) * amplitude * inv * share
        gradient_out[1] = quadratic(r0_k1, r0_k2, d2_k2) * share
        gradient_out[2] = quadratic(rr0, r0_d2, d2_d2) * share

        assert len(started) == copies_in_all, len(started)
        for copy in started:
            copy.wait_send()

    unit = (columns, width)
    scratch = [
        pltpu.VMEM((xs, zs, UNIT, width), BF16),
        pltpu.VMEM((xs, zs, *unit), F32),
        pltpu.VMEM((xs, zs, *unit), F32),
        pltpu.VMEM((gs, FEATURES, width), BF16),
        pltpu.VMEM((gs, *unit), F32),
        pltpu.VMEM((gs, *unit), F32),
        pltpu.VMEM((gs, *unit), F32),
        pltpu.VMEM((row_tiles, 128, wide), BF16),
        pltpu.VMEM((row_tiles, tiles, wide, wide), BF16),
        pltpu.VMEM((row_tiles, tiles, wide, wide), BF16),
        pltpu.VMEM((3, gs, *unit), F32),
        pltpu.VMEM((2, columns, tiles // 2 * wide), BF16),
        pltpu.VMEM((tiles, wide, width), F32),
        pltpu.VMEM((gs, *unit), F32),
        pltpu.VMEM((gs, *unit), F32),
        pltpu.VMEM((planes, 1, 128), F32),
        pltpu.VMEM((zs, 1, 128), F32),
        pltpu.VMEM((planes, 1, 128), F32),
        pltpu.VMEM((zs, 1, 128), F32),
        pltpu.SemaphoreType.DMA((4,)),
        pltpu.SemaphoreType.DMA((copies_in_all,)),
        pltpu.SemaphoreType.DMA((copies_in_all,)),
    ]
    hbm = pl.BlockSpec(memory_space=pltpu.HBM)
    vmem = pl.BlockSpec(memory_space=pltpu.VMEM)
    smem = pl.BlockSpec(memory_space=pltpu.SMEM)
    return pl.pallas_call(
        kernel,
        out_shape=(
            jax.ShapeDtypeStruct(unit, F32),
            jax.ShapeDtypeStruct(unit, F32),
            jax.ShapeDtypeStruct((3,), F32),
        ),
        in_specs=[hbm, hbm, smem, smem, smem],
        out_specs=(vmem, vmem, smem),
        scratch_shapes=scratch,
        compiler_params=pltpu.CompilerParams(
            collective_id=0, has_side_effects=True
        ),
    )


def solution(mesh):
    sizes = (4, 2, 4, 4, 2)
    split = Mesh(mesh.devices.reshape(sizes), AXES)

    def local(points, right_side, lengthscale, outputscale, noise_level):
        columns, width = right_side.shape
        call = make_kernel(sizes, columns, width, width * math.prod(sizes))
        return call(points, right_side, lengthscale, outputscale, noise_level)

    return jax.shard_map(
        local,
        mesh=split,
        in_specs=(P(None, AXES), P(None, AXES), P(), P(), P()),
        out_specs=(P(None, AXES), P(None, AXES), P()),
        check_vma=False,
    )
```

time: 81.7 us -> 67.3 us (0.82)
  Pallas kernels: 75.7 us -> 62 us
    pallas_call x1, Pallas kernels: 75.7 us -> 62 us  [local(): return call(points, right_side, lengthscale, outputscale, noise_level)]
where the time goes in v2:
time: 67.3 us; the launch traced here: 67 us
  Pallas kernels  62 us (92%)
  between operations  2.59 us (4%)
  local copies, waits for them, and re-layouts  2.42 us (4%)
    pallas_call x1, Pallas kernels, local(): return call(points, right_side, lengthscale, outputscale, noise_level)  62 us
    unnamed x7, local copies, waits for them, and re-layouts  2.42 us

profile of v2, /device:TPU:1, one launch (start us, length us, event | category | flops | bytes accessed | tf_op | source)
XLA Modules:
  0.0 67.0 jit_solution(8225304960479930497)
XLA Ops:
  2.6 62.0 %shard_map.76 = (f32[16,128]{1,0:T(8,128)}, f32[16,128]{1,0:T(8,128)}, f32[3]{0:T(128)}) custom-call(bf16[64,128]{1,0:T(8,128)(2,1)} %points_in.1, f32[16,128]{1,0:T(8,128)} %right_in.1, f32[1]{0:T(128)S(6)} %copy.11.length_in, f32[1]{0:T(128)S(6)} %copy.12.scale_in, f32[1]{0:T(128)S(6)} %copy.13.noise_in), custom_call_target="tpu_custom_call" | custom-call | tf_op jit(solution)/shard_map/pallas_call | solution.py:494
  64.6 0.0 copy-start
  64.6 1.3 %copy.14 = f32[16,128]{1,0:T(8,128)} copy(f32[16,128]{1,0:T(8,128)} %get-tuple-element.6) | data formatting | bytes 16384
  65.9 0.0 copy-done
  65.9 0.0 copy-start.1
  65.9 0.6 copy.15
  66.5 0.0 copy-done.1
  66.5 0.5 copy.16
Async XLA Ops:
  64.6 1.3 %copy-start = (f32[16,128]{1,0:T(8,128)S(1)}, f32[16,128]{1,0:T(8,128)}, u32[]{:S(2)}) copy-start(f32[16,128]{1,0:T(8,128)} %get-tuple-element.7) | copy-start | bytes 24580
  65.9 0.6 copy-start.1

commit v3 on v2

--- a/solution.py
+++ b/solution.py
@@ -203,7 +203,7 @@
             linear = root_dist * root + 1.0
             bend = dist * third
             plain = linear * damping
-            return (plain + bend * damping).astype(BF16), (bend * plain).astype(BF16)
+            return (plain + bend * damping).astype(BF16), (bend * plain * inv).astype(BF16)
 
         def add_product(part, r, product):
             acc[part, 2 * r] += product[:, :width]
@@ -270,16 +270,14 @@
         sweep(2, mid, x_tiles)
         wait(ring["right", 1])
         sweep(1, mid, x_tiles)
-        wait(z_r0)
-        ring0 = {("right", 0): ring_send(r0c, 0, 1, 1)}
-        ring_rest(r0c, ring0)
         wait(ring["left", 0])
         sweep(2, 0, mid)
         wait(ring["far", 0])
         sweep(3, 0, mid)
-        pass_right(r0c, ring0)
-        pass_left(r0c, ring0)
         wait(ring["far", 1])
+        wait(z_r0)
+        ring0 = {("right", 0): ring_send(r0c, 0, 1, 1)}
+        ring_rest(r0c, ring0)
 
         order = [r for r in range(1, row_tiles)] + [0]
         loaded = [load_tile(3, t) for t in range(mid, x_tiles)]
@@ -331,6 +329,8 @@
         plane1[0] = join(own_sums)[0:1]
         in_plane = [send(plane1.at[0], plane1.at[s], plane_peer(s)) for s in range(1, planes)]
 
+        pass_right(r0c, ring0)
+        pass_left(r0c, ring0)
         ring = {}
         wait(z_a1[: half - 1])
         ring["right", 0] = ring_send(a1c, 0, 1, 1)
@@ -383,24 +383,26 @@
 
         arriving = []
         bilinear = jnp.zeros((16, width), F32)
-        for r in order:
-            sides = []
-            slopes = jnp.zeros((16, wide), F32)
-            for side in range(2):
-                part = kmat[r, side * (tiles // 2) : (side + 1) * (tiles // 2)].reshape(tiles // 2 * wide, wide)
-                sides.append(jnp.dot(vb2[side], part, preferred_element_type=F32))
+        for both in zip(order[::2], order[1::2]):
+            totals, slopes = {}, {r: jnp.zeros((16, wide), F32) for r in both}
             for t in range(tiles):
-                for q in range(0, wide, 64):
-                    scale = upright[t, q : q + 64, :]
-                    terms = gmat[r, t, q : q + 64, :].astype(F32) * jnp.concatenate([scale, scale], axis=1)
-                    slopes = slopes + add_all([terms[i : i + 16] for i in range(0, 64, 16)])
-            total = sides[0] + sides[1]
-            for h in range(2):
-                s = 2 * r + h
-                acc[2, s] = total[:, h * width : (h + 1) * width]
-                bilinear = bilinear + slopes[:, h * width : (h + 1) * width] * d2r[s][0:1]
-                if s:
-                    arriving.append(send(acc.at[2, s], rs2.at[opposite(s)], plane_peer(opposite(s))))
+                side, place = t // (tiles // 2), t % (tiles // 2) * wide
+                vectors = vb2[side, :, place : place + wide]
+                for r in both:
+                    product = jnp.dot(vectors, kmat[r, t], preferred_element_type=F32)
+                    totals[r] = totals[r] + product if r in totals else product
+                for r in both:
+                    for q in range(0, wide, 64):
+                        scale = upright[t, q : q + 64, :]
+                        terms = gmat[r, t, q : q + 64, :].astype(F32) * jnp.concatenate([scale, scale], axis=1)
+                        slopes[r] = slopes[r] + add_all([terms[i : i + 16] for i in range(0, 64, 16)])
+            for r in both:
+                for h in range(2):
+                    s = 2 * r + h
+                    acc[2, s] = totals[r][:, h * width : (h + 1) * width]
+                    bilinear = bilinear + slopes[r][:, h * width : (h + 1) * width] * d2r[s][0:1]
+                    if s:
+                        arriving.append(send(acc.at[2, s], rs2.at[opposite(s)], plane_peer(opposite(s))))
 
         def dot_rows(left, part):
             return add_all([left[s] * acc[part, s] for s in range(gs)])
@@ -432,7 +434,7 @@
             return jnp.sum(terms[:, 0:1])
 
         share = 0.5 / total_points
-        gradient_out[0] = quadratic(r0_g1, d2_g1, d2_g2) * amplitude * inv * share
+        gradient_out[0] = quadratic(r0_g1, d2_g1, d2_g2) * amplitude * share
         gradient_out[1] = quadratic(r0_k1, r0_k2, d2_k2) * share
         gradient_out[2] = quadratic(rr0, r0_d2, d2_d2) * share
 

time: 67.3 us -> 65.3 us (0.970)
  Pallas kernels: 62 us -> 60 us
    pallas_call x1, Pallas kernels: 62 us -> 60 us  [local(): return call(points, right_side, lengthscale, outputscale, noise_level)]
where the time goes in v3:
time: 65.3 us; the launch traced here: 65 us
  Pallas kernels  60 us (92%)
  between operations  2.59 us (4%)
  local copies, waits for them, and re-layouts  2.42 us (4%)
    pallas_call x1, Pallas kernels, local(): return call(points, right_side, lengthscale, outputscale, noise_level)  60 us
    unnamed x7, local copies, waits for them, and re-layouts  2.42 us

profile of v3, /device:TPU:1, one launch (start us, length us, event | category | flops | bytes accessed | tf_op | source)
XLA Modules:
  0.0 65.0 jit_solution(7606434611470136754)
XLA Ops:
  2.6 60.0 %shard_map.76 = (f32[16,128]{1,0:T(8,128)}, f32[16,128]{1,0:T(8,128)}, f32[3]{0:T(128)}) custom-call(bf16[64,128]{1,0:T(8,128)(2,1)} %points_in.1, f32[16,128]{1,0:T(8,128)} %right_in.1, f32[1]{0:T(128)S(6)} %copy.11.length_in, f32[1]{0:T(128)S(6)} %copy.12.scale_in, f32[1]{0:T(128)S(6)} %copy.13.noise_in), custom_call_target="tpu_custom_call" | custom-call | tf_op jit(solution)/shard_map/pallas_call | solution.py:496
  62.6 0.0 copy-start
  62.6 1.3 %copy.14 = f32[16,128]{1,0:T(8,128)} copy(f32[16,128]{1,0:T(8,128)} %get-tuple-element.6) | data formatting | bytes 16384
  63.9 0.0 copy-done
  63.9 0.0 copy-start.1
  63.9 0.6 copy.15
  64.5 0.0 copy-done.1
  64.5 0.5 copy.16
Async XLA Ops:
  62.6 1.3 %copy-start = (f32[16,128]{1,0:T(8,128)S(1)}, f32[16,128]{1,0:T(8,128)}, u32[]{:S(2)}) copy-start(f32[16,128]{1,0:T(8,128)} %get-tuple-element.7) | copy-start | bytes 24580
  63.9 0.6 copy-start.1
